TPU v7x, 128 devices: a whole 4x4x4 slice. The times are simulated.
128 devices in a mesh: ka: 16 (over y, z), row: 8 (over x, core).
Axes of the slice: x: 4, y: 4, z: 4, core: 2. Of those that a mesh axis runs over, the one named last changes fastest.
Arguments:
- base_k: float32 [128, 3], P('ka'), may hold values from 0 to 1
- counts: int32 [128], P('ka'), may hold values from 1 to 4, 320 in all
- block_order: int32 [128], P(('ka', 'row')), may hold values from 0 to 127, each once
- lattice: int32 [4096, 3], P('row'), may hold values from -8 to 7, as said below
- real_space: bfloat16 [4096, 3, 128, 2, 128], P('row', None, 'ka'), may hold values from -0.09375 to 0.09375
- eigvecs: bfloat16 [512, 128, 2, 128], P(('ka', 'row')), may hold values from -0.5 to 0.5
- occupied: int32 [512, 128], P(('ka', 'row')), may hold values 0 or 1
Outputs:
- curvature: float32 [512], P(('ka', 'row'))
Inputs may be any that keep to these rules, and one draw needn't show every extreme that they name: The counts sum to 320, and some block has count 4. `block_order`: each block stands at exactly one position. `lattice`: all 4096 R-vectors are distinct.
All inputs are finite; a program needn't handle non-finite values. No bound on the sum of `occupied` on one device may be relied on, other than what follows from the above.
Results may differ from a plain program's by a relative error of at most 0.012.
The roundings to bfloat16 on the way count: a program that leaves them out, or rounds other values in their place, can miss the bound.
Values sent between devices are 32-bit elements; how exact they have to be, the bound alone decides.
No kernel may reach another device: no remote copies, remote signals or barrier semaphores. Data moves between devices by JAX's collectives and lax.ppermute only.
A program may use at most 128 MiB of HBM per device.

v0:
```python
import math
import jax
import jax.numpy as jnp
from jax import lax
from jax.sharding import Mesh
from jax.sharding import PartitionSpec as P

SUB = 4
KA = ("ka_0", "ka_1")
KA_ROW = ("ka_0", "ka_1", "row_0", "row_1")
ROW = ("row_0", "row_1")
broadening = 1.0
refine_step = (0.05, 0.03, 0.02)


def sent_to_all(value, axis):
    copies = jnp.broadcast_to(value, (lax.axis_size(axis), *value.shape))
    return lax.all_to_all(copies, axis, split_axis=0, concat_axis=0, tiled=True)


def laid_out(pieces, dim):
    lengths = list(pieces.shape[1:])
    lengths[dim] *= pieces.shape[0]
    return jnp.moveaxis(pieces, 0, dim).reshape(lengths)


def gather_directly(value, axis, dim):
    pieces = sent_to_all(value, axis)
    return laid_out(pieces, dim)


def gather_in_order(value, axes, sequence):
    pieces = value[None]
    for k in sequence:
        pieces = lax.all_gather(pieces, axes[k], axis=0, tiled=True)
    held = [lax.axis_size(axes[k]) for k in reversed(sequence)]
    pieces = pieces.reshape(*held, *value.shape)
    turned = sorted(range(len(sequence)), key=lambda place: sequence[len(sequence) - 1 - place])
    return pieces.transpose(*turned, *range(len(sequence), pieces.ndim)).reshape(-1, *value.shape)


def gathered_by_axis(value, axes, sequence, dim):
    return laid_out(gather_in_order(value, axes, sequence), dim)


def slot_points(base_points, block_counts):
    count_float = block_counts.astype(jnp.float32)
    sub_index = jnp.arange(SUB, dtype=jnp.float32)
    fraction = (sub_index[None, :] + 0.5) / count_float[:, None] - 0.5
    refine = jnp.array(refine_step, dtype=jnp.float32)
    kpoints = base_points[:, None, :] + fraction[:, :, None] * refine[None, None, :]
    alive = jnp.arange(SUB, dtype=jnp.int32)[None, :] < block_counts[:, None]
    weight = jnp.where(alive, 1.0 / count_float[:, None], 0.0)
    block_total = base_points.shape[0]
    return (kpoints.reshape(block_total * SUB, 3), weight.reshape(block_total * SUB))


def make_phases(kpoints, lattice):
    coords = lattice.astype(jnp.float32)
    angles = (
        2.0
        * math.pi
        * (
            kpoints[:, 0:1] * coords[None, :, 0]
            + kpoints[:, 1:2] * coords[None, :, 1]
            + kpoints[:, 2:3] * coords[None, :, 2]
        )
    )
    cosines = jnp.cos(angles)
    sines = jnp.sin(angles)
    coord_x = coords[None, :, 0]
    coord_y = coords[None, :, 1]
    return jnp.stack(
        [cosines, sines, -coord_x * sines, coord_x * cosines, -coord_y * sines, coord_y * cosines]
    ).astype(jnp.bfloat16)


def combine(first_part, second_part):
    real_part = first_part[..., 0, :] - second_part[..., 1, :]
    imag_part = second_part[..., 0, :] + first_part[..., 1, :]
    return jnp.stack([real_part, imag_part], axis=-2)


def fourier(kpoints, lattice, real_space):
    phase_rows = make_phases(kpoints, lattice)
    row_count = kpoints.shape[0]
    r_count = real_space.shape[0]
    slab_rows = real_space.shape[2]
    width = real_space.shape[4]
    matrix_h = real_space[:, 0].reshape(r_count, slab_rows * 2 * width)
    matrix_a = real_space[:, 1:3].reshape(r_count, 2 * slab_rows * 2 * width)
    product_h = jnp.dot(
        phase_rows.reshape(6 * row_count, r_count), matrix_h, preferred_element_type=jnp.float32
    ).reshape(6, row_count, slab_rows, 2, width)
    product_a = jnp.dot(
        phase_rows[0:2].reshape(2 * row_count, r_count),
        matrix_a,
        preferred_element_type=jnp.float32,
    ).reshape(2, row_count, 2, slab_rows, 2, width)
    pieces = [
        combine(product_h[0], product_h[1]),
        combine(product_h[2], product_h[3]),
        combine(product_h[4], product_h[5]),
        combine(product_a[0, :, 0], product_a[1, :, 0]),
        combine(product_a[0, :, 1], product_a[1, :, 1]),
    ]
    return jnp.stack(pieces, axis=1)


def curvature(k_field, vectors, occupied, weight):
    best = lax.Precision.HIGHEST
    width = k_field.shape[-1]
    vectors_f = vectors.astype(jnp.float32)
    mat_real = k_field[:, :, :, 0, :]
    mat_imag = k_field[:, :, :, 1, :]
    vec_real = vectors_f[:, :, 0, :]
    vec_imag = vectors_f[:, :, 1, :]
    turned_real = jnp.einsum("ncij,njb->ncib", mat_real, vec_real, precision=best) - jnp.einsum(
        "ncij,njb->ncib", mat_imag, vec_imag, precision=best
    )
    turned_imag = jnp.einsum("ncij,njb->ncib", mat_real, vec_imag, precision=best) + jnp.einsum(
        "ncij,njb->ncib", mat_imag, vec_real, precision=best
    )
    energy = jnp.sum(vec_real * turned_real[:, 0] + vec_imag * turned_imag[:, 0], axis=1)
    bar_real = jnp.einsum(
        "nia,ncib->ncab", vec_real, turned_real[:, 1:], precision=best
    ) + jnp.einsum("nia,ncib->ncab", vec_imag, turned_imag[:, 1:], precision=best)
    bar_imag = jnp.einsum(
        "nia,ncib->ncab", vec_real, turned_imag[:, 1:], precision=best
    ) - jnp.einsum("nia,ncib->ncab", vec_imag, turned_real[:, 1:], precision=best)
    spacing = energy[:, None, :] - energy[:, :, None]
    smoothed = spacing / (spacing * spacing + broadening)
    xcov_real = bar_real[:, 2] + smoothed * bar_real[:, 0]
    xcov_imag = bar_imag[:, 2] + smoothed * bar_imag[:, 0]
    ycov_real = bar_real[:, 3] + smoothed * bar_real[:, 1]
    ycov_imag = bar_imag[:, 3] + smoothed * bar_imag[:, 1]
    product_im = xcov_real * jnp.swapaxes(ycov_imag, 1, 2) + xcov_imag * jnp.swapaxes(
        ycov_real, 1, 2
    )
    filled = occupied.astype(jnp.float32)
    pairing = filled[:, :, None] * (1.0 - filled[:, None, :])
    berry_sum = -2.0 / width * jnp.sum(pairing * product_im, axis=(1, 2))
    return weight * berry_sum


def on_device(base_k, counts, block_order, lattice, real_space, eigvecs, occupied):
    all_base, all_counts = (gather_directly(base_k, KA, 0), gather_directly(counts, KA, 0))
    all_order = gathered_by_axis(block_order, (("ka_0", "ka_1", "row_0"), "row_1"), (0, 1), 0)
    block_total = all_order.shape[0]
    chosen = all_order[:, None] == jnp.arange(block_total, dtype=jnp.int32)[None, :]
    block_counts = jnp.sum(jnp.where(chosen, all_counts[None, :], 0), axis=1).astype(jnp.int32)
    base_points = jnp.sum(jnp.where(chosen[:, :, None], all_base[None, :, :], 0.0), axis=1)
    kpoints, weight = slot_points(base_points, block_counts)
    slot_count = kpoints.shape[0]
    ka_size = lax.axis_size(KA)
    row_size = lax.axis_size(ROW)
    per_device = slot_count // (ka_size * row_size)
    width = real_space.shape[4]
    slot_order = (
        jnp.arange(slot_count, dtype=jnp.int32)
        .reshape(ka_size, row_size, per_device)
        .transpose(1, 0, 2)
        .reshape(slot_count)
    )
    summed = lax.psum_scatter(
        fourier(kpoints[slot_order], lattice, real_space), ROW, scatter_dimension=0, tiled=True
    )
    reduced = summed.reshape((ka_size, per_device) + summed.shape[1:])
    arrived = lax.all_to_all(reduced, KA, split_axis=0, concat_axis=3, tiled=True)
    k_field = arrived.reshape(per_device, 5, width, 2, width)
    position = lax.axis_index(KA) * row_size + lax.axis_index(ROW)
    own_weight = lax.dynamic_slice_in_dim(weight, position * per_device, per_device)
    return curvature(k_field, eigvecs, occupied, own_weight)


def solution(mesh):
    finer = Mesh(mesh.devices.reshape(4, 4, 4, 2), ("ka_0", "ka_1", "row_0", "row_1"))
    placed = (
        P(KA, None),
        P(KA),
        P(KA_ROW),
        P(ROW, None),
        P(ROW, None, KA, None, None),
        P(KA_ROW, None, None, None),
        P(KA_ROW, None),
    )
    return jax.shard_map(
        on_device, mesh=finer, in_specs=placed, out_specs=P(KA_ROW), check_vma=False
    )
```

profile of v0, /device:TPU:83, one launch (start us, length us, event | category | flops | bytes accessed | tf_op | source)
XLA Modules:
  0.0 414.8 jit_solution(16123658147926405169)
XLA Ops:
  6.5 1.3 broadcast_in_dim.73
  7.8 6.8 %all-to-all-start = ((s32[16,1,8]{2,1,0:T(1,128)}), s32[16,1,8]{2,1,0:T(1,128)S(1)}, u32[]{:S(2)}, u32[]{:S(2)}) async-start(s32[16,1,8]{2,1,0:T(1,128)} %broadcast_in_dim.73), calls=%async_computation | async-start | bytes 16384 | tf_op jit(solution)/shard_map/all_to_all | solution.py:18
  14.7 7.2 %slice.203 = bf16[512,2,8,2,128]{4,3,2,1,0:T(2,128)(2,1)} slice(bf16[512,3,8,2,128]{4,3,2,1,0:T(2,128)(2,1)} %param.12), slice={[0:512], [1:3], [0:8], [0:2], [0:128]} | slice | bytes 8388608 | tf_op jit(solution)/shard_map/slice | solution.py:91
  23.1 0.8 dynamic-update-slice
  23.9 13.2 %all-reduce = s32[64]{0:T(128)S(1)} all-reduce(s32[64]{0:T(128)S(1)} %dynamic-update-slice), channel_id=2, replica_groups=mesh['ka_0'=4,'ka_1'=4,'row_0'=4,'row_1'=2] {'ka_0','ka_1','row_0'}, use_global_device_ids=true, to_apply=%add | all-reduce | flops 64 | bytes 512
  38.6 7.9 %all-reduce.1 = s32[128]{0:T(128)S(1)} all-reduce(s32[128]{0:T(128)S(1)} %dynamic-update-slice.1), channel_id=3, replica_groups=mesh['ka_0'=4,'ka_1'=4,'row_0'=4,'row_1'=2] {'row_1'}, use_global_device_ids=true, to_apply=%add.1 | all-reduce | flops 128 | bytes 1024
  47.2 2.8 reshape_squeeze.3
  50.0 11.2 %copy.186 = bf16[512,2,8,2,128]{0,4,3,2,1:T(8,128)(2,1)} copy(bf16[512,2,8,2,128]{4,3,2,1,0:T(2,128)(2,1)} %slice.203) | data formatting | bytes 8388608 | tf_op jit(solution)/shard_map/reshape | solution.py:91
  61.8 7.8 %all-to-all-start.1 = ((f32[16,8,3]{1,2,0:T(4,128)}), f32[16,8,3]{1,2,0:T(4,128)S(1)}, u32[]{:S(2)}, u32[]{:S(2)}) async-start(f32[16,8,3]{1,2,0:T(4,128)} %broadcast_in_dim.80), calls=%async_computation.1 | async-start | bytes 65536 | tf_op jit(solution)/shard_map/all_to_all | solution.py:18
  71.4 1.4 all-to-all-done.1
  73.4 1.5 gather_fusion
  75.3 4.3 %constant_dynamic-update-slice_fusion.1 = bf16[6,512,512]{2,1,0:T(8,128)(2,1)S(1)} fusion(f32[512]{0:T(512)S(1)} %bitcast.236, f32[512]{0:T(512)S(1)} %get-tuple-element.7, f32[512]{0:T(512)S(1)} %bitcast.229, f32[512]{0:T(512)S(1)} %get-tuple-element.6, f32[512]{0:T(512)S(1)} %bitcast.221, f32[512]{0:T(512)S(1)} %get-tuple-element.5), kind=kLoop, calls=%fused_computation.115 | loop fusion | flops 1835007 | bytes 536576
  79.7 5.7 %fusion.20 = (bf16[1,512,512]{2,1,0:T(8,128)(2,1)}, bf16[1,512,512]{2,1,0:T(8,128)(2,1)}) fusion(f32[512]{0:T(512)S(1)} %bitcast.237, f32[512]{0:T(512)S(1)} %get-tuple-element.7, f32[512]{0:T(512)S(1)} %bitcast.230, f32[512]{0:T(512)S(1)} %get-tuple-element.6, f32[512]{0:T(512)S(1)} %bitcast.222, f32[512]{0:T(512)S(1)} %get-tuple-element.5), kind=kLoop, calls=%fused_computation.47 | loop fusion | flops 2097152 | bytes 1060864 | tf_op jit(solution)/shard_map/convert
  85.3 4.3 %constant_dynamic-update-slice_fusion = bf16[6,512,512]{2,1,0:T(8,128)(2,1)S(1)} fusion(bf16[6,512,512]{2,1,0:T(8,128)(2,1)S(1)} %constant_dynamic-update-slice_fusion.1, f32[512]{0:T(512)S(1)} %bitcast.238, f32[512]{0:T(512)S(1)} %get-tuple-element.7, f32[512]{0:T(512)S(1)} %bitcast.231, f32[512]{0:T(512)S(1)} %get-tuple-element.6, f32[512]{0:T(512)S(1)} %bitcast.223, ...), kind=kLoop, calls=%fused_computation.114 | loop fusion | flops 1835008 | bytes 536576
  89.7 4.3 %fusion.22 = bf16[6,512,512]{2,1,0:T(8,128)(2,1)S(1)} fusion(bf16[6,512,512]{2,1,0:T(8,128)(2,1)S(1)} %constant_dynamic-update-slice_fusion, f32[512]{0:T(512)S(1)} %neg.16, f32[512]{0:T(512)S(1)} %bitcast.239, f32[512]{0:T(512)S(1)} %get-tuple-element.7, f32[512]{0:T(512)S(1)} %bitcast.232, f32[512]{0:T(512)S(1)} %get-tuple-element.6, f32[512]{0:T(512)S(1)} %bitcast.224, ...), kind=kLoop, calls=%fused_computation.49 | loop fusion | flops 2097152 | bytes 538624
  94.0 4.3 %fusion.23 = bf16[6,512,512]{2,1,0:T(8,128)(2,1)S(1)} fusion(bf16[6,512,512]{2,1,0:T(8,128)(2,1)S(1)} %fusion.22, f32[512]{0:T(512)S(1)} %bitcast.240, f32[512]{0:T(512)S(1)} %get-tuple-element.7, f32[512]{0:T(512)S(1)} %bitcast.233, f32[512]{0:T(512)S(1)} %get-tuple-element.6, f32[512]{0:T(512)S(1)} %bitcast.225, f32[512]{0:T(512)S(1)} %get-tuple-element.5), kind=kLoop, calls=%fused_computation.50 | loop fusion | flops 2097152 | bytes 536576
  98.3 4.3 %fusion.24 = bf16[6,512,512]{2,1,0:T(8,128)(2,1)S(1)} fusion(bf16[6,512,512]{2,1,0:T(8,128)(2,1)S(1)} %fusion.23, f32[512]{0:T(512)S(1)} %neg.17, f32[512]{0:T(512)S(1)} %bitcast.241, f32[512]{0:T(512)S(1)} %get-tuple-element.7, f32[512]{0:T(512)S(1)} %bitcast.234, f32[512]{0:T(512)S(1)} %get-tuple-element.6, f32[512]{0:T(512)S(1)} %bitcast.226, ...), kind=kLoop, calls=%fused_computation.51 | loop fusion | flops 2097152 | bytes 538624
  102.7 4.3 %fusion.25 = bf16[6,512,512]{2,1,0:T(8,128)(2,1)S(1)} fusion(bf16[6,512,512]{2,1,0:T(8,128)(2,1)S(1)} %fusion.24, f32[512]{0:T(512)S(1)} %bitcast.242, f32[512]{0:T(512)S(1)} %get-tuple-element.7, f32[512]{0:T(512)S(1)} %bitcast.235, f32[512]{0:T(512)S(1)} %get-tuple-element.6, f32[512]{0:T(512)S(1)} %bitcast.227, f32[512]{0:T(512)S(1)} %get-tuple-element.5), kind=kLoop, calls=%fused_computation.52 | loop fusion | flops 2097152 | bytes 536576 | tf_op jit(solution)/shard_map/stack | solution.py:73
  107.0 11.9 %fusion.73 = f32[3072,2048]{0,1:T(8,128)} fusion(bf16[3072,512]{1,0:T(8,128)(2,1)S(1)} %bitcast.243, bf16[512,2048]{1,0:T(8,128)(2,1)S(1)} %copy-done.12), kind=kOutput, calls=%fused_computation.133 | convolution fusion | flops 6442450944 | bytes 30408704 | tf_op jit(solution)/shard_map/dot_general | solution.py:92
  118.9 16.1 %fusion.65 = (f32[512,2048]{0,1:T(8,128)}, f32[512,2048]{0,1:T(8,128)}, f32[512,2048]{0,1:T(8,128)}, f32[512,2048]{0,1:T(8,128)}, f32[512,2048]{0,1:T(8,128)S(1)}, /*index=5*/f32[512,2048]{0,1:T(8,128)}) fusion(f32[3072,2048]{0,1:T(8,128)} %fusion.73), kind=kLoop, calls=%fused_computation.125 | loop fusion | bytes 50331648 | tf_op jit(solution)/shard_map/slice | solution.py:103
  135.0 1.8 fusion.70
  136.7 2.9 copy.191
  139.6 4.8 %fusion.71 = (f32[512,8,1,128]{0,3,2,1:T(8,128)}, f32[512,8,1,128]{0,3,2,1:T(8,128)}) fusion(f32[512,8,2,128]{0,3,2,1:T(8,128)} %bitcast.215), kind=kLoop, calls=%fused_computation.131 | loop fusion | bytes 8388608 | tf_op jit(solution)/shard_map/slice | solution.py:79
  144.5 2.9 copy.192
  147.4 2.9 copy.189
  150.3 1.8 copy.190
  152.1 4.2 %fusion.68 = (f32[512,8,1,128]{0,3,2,1:T(8,128)S(1)}, f32[512,8,1,128]{0,3,2,1:T(8,128)}) fusion(f32[512,8,2,128]{0,3,2,1:T(8,128)} %bitcast.214), kind=kLoop, calls=%fused_computation.128 | loop fusion | bytes 8388608 | tf_op jit(solution)/shard_map/slice | solution.py:79
  156.4 3.0 copy.195
  159.3 4.8 %fusion.69 = (f32[512,8,1,128]{0,3,2,1:T(8,128)}, f32[512,8,1,128]{0,3,2,1:T(8,128)}) fusion(f32[512,8,2,128]{0,3,2,1:T(8,128)} %bitcast.213), kind=kLoop, calls=%fused_computation.129 | loop fusion | bytes 8388608 | tf_op jit(solution)/shard_map/slice | solution.py:79
  164.1 2.9 copy.196
  167.0 2.9 copy.193
  169.9 1.8 copy.194
  171.7 4.2 %fusion.66 = (f32[512,8,1,128]{0,3,2,1:T(8,128)S(1)}, f32[512,8,1,128]{0,3,2,1:T(8,128)}) fusion(f32[512,8,2,128]{0,3,2,1:T(8,128)} %bitcast.212), kind=kLoop, calls=%fused_computation.126 | loop fusion | bytes 8388608 | tf_op jit(solution)/shard_map/slice | solution.py:79
  175.9 2.9 copy.199
  178.8 4.8 %fusion.67 = (f32[512,8,1,128]{0,3,2,1:T(8,128)}, f32[512,8,1,128]{0,3,2,1:T(8,128)}) fusion(f32[512,8,2,128]{0,3,2,1:T(8,128)} %bitcast.211), kind=kLoop, calls=%fused_computation.127 | loop fusion | bytes 8388608 | tf_op jit(solution)/shard_map/slice | solution.py:79
  183.6 2.9 copy.200
  186.6 2.9 copy.197
  189.5 1.8 copy.198
  191.3 6.4 %fusion.5 = f32[2,512,2,8,2,128]{5,1,4,3,2,0:T(8,128)S(1)} fusion(bf16[512,2,8,2,128]{0,4,3,2,1:T(8,128)(2,1)} %copy.186, bf16[1,512,512]{2,1,0:T(8,128)(2,1)S(1)} %copy-done.14, bf16[1,512,512]{2,1,0:T(8,128)(2,1)S(1)} %copy-done.13), kind=kOutput, calls=%fused_computation.15 | convolution fusion | flops 4297064448 | bytes 22020096 | tf_op jit(solution)/shard_map/dot_general | solution.py:95
  197.7 4.8 %slice_bitcast_fusion = (f32[512,8,2,128]{3,0,2,1:T(8,128)S(1)}, f32[512,8,2,128]{3,0,2,1:T(8,128)}, f32[512,8,2,128]{3,0,2,1:T(8,128)}, f32[512,8,2,128]{3,0,2,1:T(8,128)}) fusion(f32[2,512,2,8,2,128]{5,1,4,3,2,0:T(8,128)S(1)} %fusion.5), kind=kLoop, calls=%fused_computation.1 | loop fusion | bytes 33554432 | tf_op jit(solution)/shard_map/squeeze | solution.py:105
  202.5 2.6 add.198
  206.2 2.4 fusion
  208.6 1.3 copy-done.3
  210.1 1.4 copy-done.4
  212.3 1.4 copy-done.6
  214.6 1.4 copy-done.8
  216.8 2.3 fusion.1
  219.0 2.3 fusion.2
  221.3 8.4 %slice_subtract_fusion = (f32[512,8,1,128]{3,0,2,1:T(8,128)}, f32[512,8,1,128]{3,0,2,1:T(8,128)}, f32[512,8,1,128]{3,0,2,1:T(8,128)}, f32[512,8,1,128]{3,0,2,1:T(8,128)}) fusion(f32[512,8,2,128]{3,0,2,1:T(8,128)S(1)} %get-tuple-element.14, f32[512,8,2,128]{3,0,2,1:T(8,128)} %get-tuple-element.15, f32[512,8,2,128]{3,0,2,1:T(8,128)} %get-tuple-element.17, ...), kind=kLoop, calls=%fused_computation.19 | loop fusion | flops 2097152 | bytes 25165824 | tf_op jit(solution)/shard_map/sub | solution.py:79
  229.7 4.7 %fusion.3 = f32[512,5,8,2,128]{4,0,3,2,1:T(8,128)} fusion(f32[512,5,8,2,128]{4,0,3,2,1:T(8,128)} %fusion.2, f32[512,8,1,128]{3,0,2,1:T(8,128)} %get-tuple-element.45, f32[512,8,1,128]{3,0,2,1:T(8,128)} %get-tuple-element.46), kind=kLoop, calls=%fused_computation.12 | loop fusion | flops 1048576 | bytes 8388608
  234.4 2.2 fusion.4
  236.6 111.7 %reduce-scatter.2.cloned.1.call-done = f32[64,5,8,2,128]{4,0,3,2,1:T(8,128)} async-done(((f32[512,5,8,2,128]{4,0,3,2,1:T(8,128)}), f32[64,5,8,2,128]{4,0,3,2,1:T(8,128)}) %reduce-scatter.2.cloned.1.call-update) | async-done | bytes 2621456 | tf_op jit(solution)/shard_map/reduce_scatter | solution.py:165
  348.3 4.0 copy.155
  352.3 6.8 %all-to-all-start.2 = ((f32[16,4,5,8,2,128]{5,1,4,3,2,0:T(4,128)}), f32[16,4,5,8,2,128]{5,1,4,3,2,0:T(4,128)S(1)}, u32[]{:S(2)}, u32[]{:S(2)}) async-start(f32[16,4,5,8,2,128]{5,1,4,3,2,0:T(4,128)} %copy.155), calls=%async_computation.3 | async-start | bytes 5242880 | tf_op jit(solution)/shard_map/all_to_all | solution.py:169
  359.2 1.0 copy_convert_fusion
  360.4 37.9 %all-to-all-done.2 = f32[16,4,5,8,2,128]{5,1,4,3,2,0:T(4,128)S(1)} async-done(((f32[16,4,5,8,2,128]{5,1,4,3,2,0:T(4,128)}), f32[16,4,5,8,2,128]{5,1,4,3,2,0:T(4,128)S(1)}, u32[]{:S(2)}, u32[]{:S(2)}) %all-to-all-start.2) | async-done | bytes 2621472 | tf_op jit(solution)/shard_map/all_to_all | solution.py:169
  399.2 0.7 fusion.47
  399.9 0.7 fusion.10
  400.7 0.8 convolution_add_fusion
  401.4 1.0 fusion.16
  402.4 0.8 convolution_subtract_fusion
  403.2 1.0 fusion.14
  404.3 1.0 fusion.8
  405.4 1.0 fusion.7
  (97 shorter events, 11.7 us)
Async XLA Ops:
  7.8 53.4 %all-to-all-start = ((s32[16,1,8]{2,1,0:T(1,128)}), s32[16,1,8]{2,1,0:T(1,128)S(1)}, u32[]{:S(2)}, u32[]{:S(2)}) async-start(s32[16,1,8]{2,1,0:T(1,128)} %broadcast_in_dim.73), calls=%async_computation | async-start | bytes 16384 | tf_op jit(solution)/shard_map/all_to_all | solution.py:18
  14.6 7.2 %copy-start.15 = (s32[512,3]{0,1:T(4,128)S(1)}, s32[512,3]{0,1:T(4,128)}, u32[]{:S(2)}) copy-start(s32[512,3]{0,1:T(4,128)} %param.11) | copy-start | bytes 18436
  14.7 7.9 %copy-start.20 = (u32[128]{0:T(128)S(1)}, u32[128]{0:T(128)}, u32[]{:S(2)}) copy-start(u32[128]{0:T(128)} %constant.56) | copy-start | bytes 1540
  14.7 22.5 %copy-start.19 = (u32[128]{0:T(128)S(1)}, u32[128]{0:T(128)}, u32[]{:S(2)}) copy-start(u32[128]{0:T(128)} %constant.61) | copy-start | bytes 1540
  14.7 32.5 %slice-start = ((bf16[512,3,8,2,128]{4,3,2,1,0:T(2,128)(2,1)}), bf16[512,1,8,2,128]{4,3,2,1,0:T(2,128)(2,1)S(1)}, s32[]{:S(2)}) async-start(bf16[512,3,8,2,128]{4,3,2,1,0:T(2,128)(2,1)} %param.12), calls=%async_computation.5 | async-start | bytes 4194304 | tf_op jit(solution)/shard_map/slice | solution.py:90
  50.0 11.2 %copy-start.17 = (f32[8,3]{0,1:T(4,128)S(1)}, f32[8,3]{0,1:T(4,128)}, u32[]{:S(2)}) copy-start(f32[8,3]{0,1:T(4,128)} %param.8) | copy-start | bytes 292
  50.0 23.2 %copy-start.18 = (f32[3]{0:T(128)S(1)}, f32[3]{0:T(128)}, u32[]{:S(2)}) copy-start(f32[3]{0:T(128)} %constant.47.clone) | copy-start | bytes 40
  61.8 11.0 %all-to-all-start.1 = ((f32[16,8,3]{1,2,0:T(4,128)}), f32[16,8,3]{1,2,0:T(4,128)S(1)}, u32[]{:S(2)}, u32[]{:S(2)}) async-start(f32[16,8,3]{1,2,0:T(4,128)} %broadcast_in_dim.80), calls=%async_computation.1 | async-start | bytes 65536 | tf_op jit(solution)/shard_map/all_to_all | solution.py:18
  69.7 278.7 %reduce-scatter.2.cloned.1.call-start = ((), (), s32[]{:S(2)}) async-start(), calls=%async_computation.4 | async-start | bytes 23592960 | tf_op jit(solution)/shard_map/reduce_scatter | solution.py:165
  75.3 31.7 %copy-start.12 = (bf16[512,2048]{1,0:T(8,128)(2,1)S(1)}, bf16[512,2048]{1,0:T(8,128)(2,1)}, u32[]{:S(2)}) copy-start(bf16[512,2048]{1,0:T(8,128)(2,1)} %reshape_squeeze.3) | copy-start | bytes 6291460
  189.5 1.8 copy-start.13
  189.5 1.8 copy-start.14
  202.5 2.9 copy-start
  202.5 3.5 copy-start.1
  206.2 2.4 copy-start.2
  206.2 3.7 copy-start.3
  209.9 1.6 copy-start.4
  209.9 2.2 copy-start.5
  212.1 1.6 copy-start.6
  212.1 2.2 copy-start.7
  214.3 1.6 copy-start.8
  214.4 2.2 copy-start.9
  229.7 4.7 %copy-start.10 = (f32[512,8,1,128]{3,0,2,1:T(8,128)S(1)}, f32[512,8,1,128]{3,0,2,1:T(8,128)}, u32[]{:S(2)}) copy-start(f32[512,8,1,128]{3,0,2,1:T(8,128)} %get-tuple-element.18) | copy-start | bytes 6291460
  229.7 4.7 %copy-start.11 = (f32[512,8,1,128]{3,0,2,1:T(8,128)S(1)}, f32[512,8,1,128]{3,0,2,1:T(8,128)}, u32[]{:S(2)}) copy-start(f32[512,8,1,128]{3,0,2,1:T(8,128)} %get-tuple-element.19) | copy-start | bytes 6291460
  352.3 6.8 %copy-start.16 = (s32[4,128]{1,0:T(4,128)S(1)}, s32[4,128]{1,0:T(4,128)}, u32[]{:S(2)}) copy-start(s32[4,128]{1,0:T(4,128)} %param.14) | copy-start | bytes 6148
  352.3 46.0 %all-to-all-start.2 = ((f32[16,4,5,8,2,128]{5,1,4,3,2,0:T(4,128)}), f32[16,4,5,8,2,128]{5,1,4,3,2,0:T(4,128)S(1)}, u32[]{:S(2)}, u32[]{:S(2)}) async-start(f32[16,4,5,8,2,128]{5,1,4,3,2,0:T(4,128)} %copy.155), calls=%async_computation.3 | async-start | bytes 5242880 | tf_op jit(solution)/shard_map/all_to_all | solution.py:169
Sparse Core Ops, SparseCore 0:
  236.8 111.5 reduce-scatter.1
where the time goes:
time: 420 us; the launch traced here: 415 us
  waiting for transfers between devices  151 us (36%)
  local copies, waits for them, and re-layouts  119 us (28%)
  other arithmetic  61 us (15%)
  matrix products  25.3 us (6%)
  starting transfers between devices  21.5 us (5%)
  blocking collectives  21.1 us (5%)
  between operations  15.4 us (4%)
    reduce_scatter x1, waiting for transfers between devices, on_device(): lax.psum_scatter(fourier(kpoints[slot_order], lattice, real_space), ROW,...  112 us
    unnamed x60, local copies, waits for them, and re-layouts  42.1 us
    all_to_all x1, waiting for transfers between devices, on_device(): lax.all_to_all(reduced, KA, split_axis=0, concat_axis=3, tiled=True)  37.9 us
    unnamed x9, other arithmetic  33.3 us
    slice x6, local copies, waits for them, and re-layouts, combine(): real_part = first_part[..., 0, :] - second_part[..., 1, :]  24.6 us
    unnamed x2, blocking collectives  21.1 us
    slice x1, local copies, waits for them, and re-layouts, fourier(): product_h[4]  16.1 us
    all_to_all x2, starting transfers between devices, sent_to_all(): return lax.all_to_all(copies, axis, split_axis=0, concat_axis=0, tiled=True)  14.7 us
  transfers between devices with their start and end apart: 4, of which 3 were waited for; matrix products, arithmetic and copies ran while one was open for 6% of the time, Pallas kernels for 0%

commit v1 on v0

--- a/solution.py
+++ b/solution.py
@@ -4,6 +4,7 @@
 from jax import lax
 from jax.sharding import Mesh
 from jax.sharding import PartitionSpec as P
+from jax.lax import all_to_all, axis_size
 
 SUB = 4
 KA = ("ka_0", "ka_1")
@@ -166,7 +167,12 @@
         fourier(kpoints[slot_order], lattice, real_space), ROW, scatter_dimension=0, tiled=True
     )
     reduced = summed.reshape((ka_size, per_device) + summed.shape[1:])
-    arrived = lax.all_to_all(reduced, KA, split_axis=0, concat_axis=3, tiled=True)
+    arrived = jnp.concatenate(
+        all_to_all(
+            jnp.stack(jnp.split(reduced, axis_size(KA), axis=0)), KA, split_axis=0, concat_axis=0
+        ),
+        axis=3,
+    )
     k_field = arrived.reshape(per_device, 5, width, 2, width)
     position = lax.axis_index(KA) * row_size + lax.axis_index(ROW)
     own_weight = lax.dynamic_slice_in_dim(weight, position * per_device, per_device)

time: 420 us -> 444 us (1.057)
  local copies, waits for them, and re-layouts: 119 us -> 142 us
    unnamed x60 -> x75, local copies, waits for them, and re-layouts: 42.1 us -> 67 us
where the time goes in v1:
time: 444 us; the launch traced here: 437 us
  waiting for transfers between devices  151 us (34%)
  local copies, waits for them, and re-layouts  142 us (32%)
  other arithmetic  61 us (14%)
  matrix products  25.3 us (6%)
  starting transfers between devices  21.5 us (5%)
  blocking collectives  21.1 us (5%)
  between operations  15.5 us (3%)
    reduce_scatter x1, waiting for transfers between devices, on_device(): lax.psum_scatter(fourier(kpoints[slot_order], lattice, real_space), ROW,...  112 us
    unnamed x75, local copies, waits for them, and re-layouts  67 us
    all_to_all x1, waiting for transfers between devices, on_device(): all_to_all(jnp.stack(jnp.split(reduced, axis_size(KA), axis=0)), KA, spli...  37.9 us
    unnamed x9, other arithmetic  33.3 us
    slice x6, local copies, waits for them, and re-layouts, combine(): real_part = first_part[..., 0, :] - second_part[..., 1, :]  24.6 us
    unnamed x2, blocking collectives  21.1 us
    slice x1, local copies, waits for them, and re-layouts, fourier(): product_h[4]  16.1 us
    all_to_all x2, starting transfers between devices, sent_to_all(): return lax.all_to_all(copies, axis, split_axis=0, concat_axis=0, tiled=True)  14.7 us
  transfers between devices with their start and end apart: 4, of which 3 were waited for; matrix products, arithmetic and copies ran while one was open for 6% of the time, Pallas kernels for 0%

profile of v1, /device:TPU:83, one launch (start us, length us, event | category | flops | bytes accessed | tf_op | source)
XLA Modules:
  0.0 437.5 jit_solution(16898575967570664315)
XLA Ops:
  7.8 6.8 %all-to-all-start = ((s32[16,1,8]{2,1,0:T(1,128)}), s32[16,1,8]{2,1,0:T(1,128)S(1)}, u32[]{:S(2)}, u32[]{:S(2)}) async-start(s32[16,1,8]{2,1,0:T(1,128)} %broadcast_in_dim.73), calls=%async_computation | async-start | bytes 16384 | tf_op jit(solution)/shard_map/all_to_all | solution.py:19
  14.7 7.2 %slice.219 = bf16[512,2,8,2,128]{4,3,2,1,0:T(2,128)(2,1)} slice(bf16[512,3,8,2,128]{4,3,2,1,0:T(2,128)(2,1)} %param.12), slice={[0:512], [1:3], [0:8], [0:2], [0:128]} | slice | bytes 8388608 | tf_op jit(solution)/shard_map/slice | solution.py:92
  23.9 13.2 %all-reduce = s32[64]{0:T(128)S(1)} all-reduce(s32[64]{0:T(128)S(1)} %dynamic-update-slice), channel_id=2, replica_groups=mesh['ka_0'=4,'ka_1'=4,'row_0'=4,'row_1'=2] {'ka_0','ka_1','row_0'}, use_global_device_ids=true, to_apply=%add | all-reduce | flops 64 | bytes 512
  38.6 7.9 %all-reduce.1 = s32[128]{0:T(128)S(1)} all-reduce(s32[128]{0:T(128)S(1)} %dynamic-update-slice.1), channel_id=3, replica_groups=mesh['ka_0'=4,'ka_1'=4,'row_0'=4,'row_1'=2] {'row_1'}, use_global_device_ids=true, to_apply=%add.1 | all-reduce | flops 128 | bytes 1024
  47.2 2.8 reshape_squeeze.3
  50.0 11.2 %copy.190 = bf16[512,2,8,2,128]{0,4,3,2,1:T(8,128)(2,1)} copy(bf16[512,2,8,2,128]{4,3,2,1,0:T(2,128)(2,1)} %slice.219) | data formatting | bytes 8388608 | tf_op jit(solution)/shard_map/reshape | solution.py:92
  61.8 7.8 %all-to-all-start.1 = ((f32[16,8,3]{1,2,0:T(4,128)}), f32[16,8,3]{1,2,0:T(4,128)S(1)}, u32[]{:S(2)}, u32[]{:S(2)}) async-start(f32[16,8,3]{1,2,0:T(4,128)} %broadcast_in_dim.80), calls=%async_computation.1 | async-start | bytes 65536 | tf_op jit(solution)/shard_map/all_to_all | solution.py:19
  71.4 1.4 all-to-all-done.1
  73.4 1.5 gather_fusion
  75.3 4.3 constant_dynamic-update-slice_fusion.1
  79.7 5.7 %fusion.20 = (bf16[1,512,512]{2,1,0:T(8,128)(2,1)}, bf16[1,512,512]{2,1,0:T(8,128)(2,1)}) fusion(f32[512]{0:T(512)S(1)} %bitcast.299, f32[512]{0:T(512)S(1)} %get-tuple-element.7, f32[512]{0:T(512)S(1)} %bitcast.292, f32[512]{0:T(512)S(1)} %get-tuple-element.6, f32[512]{0:T(512)S(1)} %bitcast.284, f32[512]{0:T(512)S(1)} %get-tuple-element.5), kind=kLoop, calls=%fused_computation.47 | loop fusion | flops 2097152 | bytes 1060864 | tf_op jit(solution)/shard_map/convert
  85.3 4.3 constant_dynamic-update-slice_fusion
  89.7 4.3 fusion.22
  94.0 4.3 fusion.23
  98.3 4.3 fusion.24
  102.7 4.3 fusion.25
  107.0 11.9 %fusion.89 = f32[3072,2048]{0,1:T(8,128)} fusion(bf16[3072,512]{1,0:T(8,128)(2,1)S(1)} %bitcast.305, bf16[512,2048]{1,0:T(8,128)(2,1)S(1)} %copy-done.12), kind=kOutput, calls=%fused_computation.165 | convolution fusion | flops 6442450944 | bytes 30408704 | tf_op jit(solution)/shard_map/dot_general | solution.py:93
  118.9 16.1 %fusion.81 = (f32[512,2048]{0,1:T(8,128)}, f32[512,2048]{0,1:T(8,128)}, f32[512,2048]{0,1:T(8,128)}, f32[512,2048]{0,1:T(8,128)}, f32[512,2048]{0,1:T(8,128)S(1)}, /*index=5*/f32[512,2048]{0,1:T(8,128)}) fusion(f32[3072,2048]{0,1:T(8,128)} %fusion.89), kind=kLoop, calls=%fused_computation.157 | loop fusion | bytes 50331648 | tf_op jit(solution)/shard_map/slice | solution.py:104
  135.0 1.8 fusion.86
  136.7 2.9 copy.197
  139.6 4.8 %fusion.87 = (f32[512,8,1,128]{0,3,2,1:T(8,128)}, f32[512,8,1,128]{0,3,2,1:T(8,128)}) fusion(f32[512,8,2,128]{0,3,2,1:T(8,128)} %bitcast.278), kind=kLoop, calls=%fused_computation.163 | loop fusion | bytes 8388608 | tf_op jit(solution)/shard_map/slice | solution.py:80
  144.5 2.9 copy.198
  147.4 2.9 copy.195
  150.3 1.8 copy.196
  152.1 4.2 fusion.84
  156.4 3.0 copy.201
  159.3 4.8 %fusion.85 = (f32[512,8,1,128]{0,3,2,1:T(8,128)}, f32[512,8,1,128]{0,3,2,1:T(8,128)}) fusion(f32[512,8,2,128]{0,3,2,1:T(8,128)} %bitcast.276), kind=kLoop, calls=%fused_computation.161 | loop fusion | bytes 8388608 | tf_op jit(solution)/shard_map/slice | solution.py:80
  164.1 2.9 copy.202
  167.0 2.9 copy.199
  169.9 1.8 copy.200
  171.7 4.2 fusion.82
  175.9 2.9 copy.205
  178.8 4.8 %fusion.83 = (f32[512,8,1,128]{0,3,2,1:T(8,128)}, f32[512,8,1,128]{0,3,2,1:T(8,128)}) fusion(f32[512,8,2,128]{0,3,2,1:T(8,128)} %bitcast.274), kind=kLoop, calls=%fused_computation.159 | loop fusion | bytes 8388608 | tf_op jit(solution)/shard_map/slice | solution.py:80
  183.6 2.9 copy.206
  186.6 2.9 copy.203
  189.5 1.8 copy.204
  191.3 6.4 %fusion.5 = f32[2,512,2,8,2,128]{5,1,4,3,2,0:T(8,128)S(1)} fusion(bf16[512,2,8,2,128]{0,4,3,2,1:T(8,128)(2,1)} %copy.190, bf16[1,512,512]{2,1,0:T(8,128)(2,1)S(1)} %copy-done.14, bf16[1,512,512]{2,1,0:T(8,128)(2,1)S(1)} %copy-done.13), kind=kOutput, calls=%fused_computation.15 | convolution fusion | flops 4297064448 | bytes 22020096 | tf_op jit(solution)/shard_map/dot_general | solution.py:96
  197.7 4.8 %slice_bitcast_fusion = (f32[512,8,2,128]{3,0,2,1:T(8,128)S(1)}, f32[512,8,2,128]{3,0,2,1:T(8,128)}, f32[512,8,2,128]{3,0,2,1:T(8,128)}, f32[512,8,2,128]{3,0,2,1:T(8,128)}) fusion(f32[2,512,2,8,2,128]{5,1,4,3,2,0:T(8,128)S(1)} %fusion.5), kind=kLoop, calls=%fused_computation.1 | loop fusion | bytes 33554432 | tf_op jit(solution)/shard_map/squeeze | solution.py:106
  202.5 2.6 add.198
  206.2 2.4 fusion
  216.8 2.3 fusion.1
  219.0 2.3 fusion.2
  221.3 8.4 %slice_subtract_fusion = (f32[512,8,1,128]{3,0,2,1:T(8,128)}, f32[512,8,1,128]{3,0,2,1:T(8,128)}, f32[512,8,1,128]{3,0,2,1:T(8,128)}, f32[512,8,1,128]{3,0,2,1:T(8,128)}) fusion(f32[512,8,2,128]{3,0,2,1:T(8,128)S(1)} %get-tuple-element.14, f32[512,8,2,128]{3,0,2,1:T(8,128)} %get-tuple-element.15, f32[512,8,2,128]{3,0,2,1:T(8,128)} %get-tuple-element.17, ...), kind=kLoop, calls=%fused_computation.19 | loop fusion | flops 2097152 | bytes 25165824 | tf_op jit(solution)/shard_map/sub | solution.py:80
  229.7 4.7 %fusion.3 = f32[512,5,8,2,128]{4,0,3,2,1:T(8,128)} fusion(f32[512,5,8,2,128]{4,0,3,2,1:T(8,128)} %fusion.2, f32[512,8,1,128]{3,0,2,1:T(8,128)} %get-tuple-element.45, f32[512,8,1,128]{3,0,2,1:T(8,128)} %get-tuple-element.46), kind=kLoop, calls=%fused_computation.12 | loop fusion | flops 1048576 | bytes 8388608
  234.4 2.2 fusion.4
  236.6 111.7 %reduce-scatter.2.cloned.1.call-done = f32[64,5,8,2,128]{4,0,3,2,1:T(8,128)} async-done(((f32[512,5,8,2,128]{4,0,3,2,1:T(8,128)}), f32[64,5,8,2,128]{4,0,3,2,1:T(8,128)}) %reduce-scatter.2.cloned.1.call-update) | async-done | bytes 2621456 | tf_op jit(solution)/shard_map/reduce_scatter | solution.py:166
  348.3 1.7 fusion.61
  350.0 1.7 fusion.60
  351.7 1.6 fusion.59
  353.3 1.7 fusion.58
  355.0 1.7 fusion.57
  356.7 1.7 fusion.56
  358.3 1.7 fusion.55
  360.0 1.7 fusion.54
  361.7 1.6 fusion.53
  363.3 1.7 fusion.52
  365.0 1.7 fusion.51
  366.7 1.7 fusion.50
  368.4 1.7 fusion.49
  370.0 1.7 fusion.48
  371.7 1.6 fusion.47
  373.3 1.7 fusion.46
  375.0 6.8 %all-to-all-start.2 = ((f32[16,1,4,5,8,2,128]{6,2,5,4,3,1,0:T(4,128)}), f32[16,1,4,5,8,2,128]{6,2,5,4,3,1,0:T(4,128)S(1)}, u32[]{:S(2)}, u32[]{:S(2)}) async-start(f32[16,1,4,5,8,2,128]{6,2,5,4,3,1,0:T(4,128)} %fusion.46), calls=%async_computation.3 | async-start | bytes 5242880 | tf_op jit(solution)/shard_map/all_to_all | solution.py:171
  383.1 37.9 %all-to-all-done.2 = f32[16,1,4,5,8,2,128]{6,2,5,4,3,1,0:T(4,128)S(1)} async-done(((f32[16,1,4,5,8,2,128]{6,2,5,4,3,1,0:T(4,128)}), f32[16,1,4,5,8,2,128]{6,2,5,4,3,1,0:T(4,128)S(1)}, u32[]{:S(2)}, u32[]{:S(2)}) %all-to-all-start.2) | async-done | bytes 2621472 | tf_op jit(solution)/shard_map/all_to_all | solution.py:171
  (112 shorter events, 27.2 us)
Async XLA Ops:
  7.8 53.4 %all-to-all-start = ((s32[16,1,8]{2,1,0:T(1,128)}), s32[16,1,8]{2,1,0:T(1,128)S(1)}, u32[]{:S(2)}, u32[]{:S(2)}) async-start(s32[16,1,8]{2,1,0:T(1,128)} %broadcast_in_dim.73), calls=%async_computation | async-start | bytes 16384 | tf_op jit(solution)/shard_map/all_to_all | solution.py:19
  14.6 7.2 %copy-start.15 = (s32[512,3]{0,1:T(4,128)S(1)}, s32[512,3]{0,1:T(4,128)}, u32[]{:S(2)}) copy-start(s32[512,3]{0,1:T(4,128)} %param.11) | copy-start | bytes 18436
  14.7 7.9 %copy-start.20 = (u32[128]{0:T(128)S(1)}, u32[128]{0:T(128)}, u32[]{:S(2)}) copy-start(u32[128]{0:T(128)} %constant.56) | copy-start | bytes 1540
  14.7 22.5 %copy-start.19 = (u32[128]{0:T(128)S(1)}, u32[128]{0:T(128)}, u32[]{:S(2)}) copy-start(u32[128]{0:T(128)} %constant.61) | copy-start | bytes 1540
  14.7 32.5 %slice-start = ((bf16[512,3,8,2,128]{4,3,2,1,0:T(2,128)(2,1)}), bf16[512,1,8,2,128]{4,3,2,1,0:T(2,128)(2,1)S(1)}, s32[]{:S(2)}) async-start(bf16[512,3,8,2,128]{4,3,2,1,0:T(2,128)(2,1)} %param.12), calls=%async_computation.5 | async-start | bytes 4194304 | tf_op jit(solution)/shard_map/slice | solution.py:91
  50.0 11.2 %copy-start.17 = (f32[8,3]{0,1:T(4,128)S(1)}, f32[8,3]{0,1:T(4,128)}, u32[]{:S(2)}) copy-start(f32[8,3]{0,1:T(4,128)} %param.8) | copy-start | bytes 292
  50.0 23.2 %copy-start.18 = (f32[3]{0:T(128)S(1)}, f32[3]{0:T(128)}, u32[]{:S(2)}) copy-start(f32[3]{0:T(128)} %constant.47.clone) | copy-start | bytes 40
  61.8 11.0 %all-to-all-start.1 = ((f32[16,8,3]{1,2,0:T(4,128)}), f32[16,8,3]{1,2,0:T(4,128)S(1)}, u32[]{:S(2)}, u32[]{:S(2)}) async-start(f32[16,8,3]{1,2,0:T(4,128)} %broadcast_in_dim.80), calls=%async_computation.1 | async-start | bytes 65536 | tf_op jit(solution)/shard_map/all_to_all | solution.py:19
  69.7 278.7 %reduce-scatter.2.cloned.1.call-start = ((), (), s32[]{:S(2)}) async-start(), calls=%async_computation.4 | async-start | bytes 23592960 | tf_op jit(solution)/shard_map/reduce_scatter | solution.py:166
  74.9 32.1 %copy-start.12 = (bf16[512,2048]{1,0:T(8,128)(2,1)S(1)}, bf16[512,2048]{1,0:T(8,128)(2,1)}, u32[]{:S(2)}) copy-start(bf16[512,2048]{1,0:T(8,128)(2,1)} %reshape_squeeze.3) | copy-start | bytes 6291460
  189.5 1.8 copy-start.13
  189.5 1.8 copy-start.14
  202.5 2.9 copy-start
  202.5 3.5 copy-start.1
  206.2 2.4 copy-start.2
  206.2 3.7 copy-start.3
  209.9 1.6 copy-start.4
  209.9 2.2 copy-start.5
  212.1 1.6 copy-start.6
  212.1 2.2 copy-start.7
  214.3 1.6 copy-start.8
  214.4 2.2 copy-start.9
  229.7 4.7 %copy-start.10 = (f32[512,8,1,128]{3,0,2,1:T(8,128)S(1)}, f32[512,8,1,128]{3,0,2,1:T(8,128)}, u32[]{:S(2)}) copy-start(f32[512,8,1,128]{3,0,2,1:T(8,128)} %get-tuple-element.18) | copy-start | bytes 6291460
  229.7 4.7 %copy-start.11 = (f32[512,8,1,128]{3,0,2,1:T(8,128)S(1)}, f32[512,8,1,128]{3,0,2,1:T(8,128)}, u32[]{:S(2)}) copy-start(f32[512,8,1,128]{3,0,2,1:T(8,128)} %get-tuple-element.19) | copy-start | bytes 6291460
  375.0 6.8 %copy-start.16 = (s32[4,128]{1,0:T(4,128)S(1)}, s32[4,128]{1,0:T(4,128)}, u32[]{:S(2)}) copy-start(s32[4,128]{1,0:T(4,128)} %param.14) | copy-start | bytes 6148
  375.0 46.0 %all-to-all-start.2 = ((f32[16,1,4,5,8,2,128]{6,2,5,4,3,1,0:T(4,128)}), f32[16,1,4,5,8,2,128]{6,2,5,4,3,1,0:T(4,128)S(1)}, u32[]{:S(2)}, u32[]{:S(2)}) async-start(f32[16,1,4,5,8,2,128]{6,2,5,4,3,1,0:T(4,128)} %fusion.46), calls=%async_computation.3 | async-start | bytes 5242880 | tf_op jit(solution)/shard_map/all_to_all | solution.py:171
Sparse Core Ops, SparseCore 0:
  236.8 111.5 reduce-scatter.1
